TPU v7x, 128 devices: a whole 4x4x4 slice. The times are simulated.
128 devices in a mesh: dp: 32 (over x, z, core), tp: 4 (over y).
Axes of the slice: x: 4, y: 4, z: 4, core: 2. Of those that a mesh axis runs over, the one named last changes fastest.
Arguments:
- hidden_in: bfloat16 [2048, 3584], P(('dp', 'tp')), may hold values from -6 to 6
- query_latent: bfloat16 [2048, 64, 512], P(('dp', 'tp')), may hold values from -348 to 347
- query_rope: bfloat16 [2048, 4096], P(('dp', 'tp')), may hold values from -348 to 347
- cache_latent: bfloat16 [2048, 128, 512], P(('dp', 'tp')), may hold values from -6 to 6
- cache_rope: bfloat16 [2048, 64, 128], P(('dp', 'tp')), may hold values from -6 to 6
- lengths: int32 [2048], P(('dp', 'tp')), may hold values from 16 to 128
- value_up: bfloat16 [512, 4096], P(None, 'tp'), may hold values from -1 to 1
- out_proj: bfloat16 [4096, 3584], P('tp'), may hold values from -0.09375 to 0.09375
- norm_gain: float32 [3584], replicated, may hold values from 0.1 to 1.9
- expert_gate: bfloat16 [128, 3584, 1024], P(('dp', 'tp')), may hold values from -0.09375 to 0.09375
- expert_down: bfloat16 [128, 1024, 3584], P(('dp', 'tp')), may hold values from -0.1875 to 0.1875
- expert_ids: int32 [2048, 8], P(('dp', 'tp')), may hold values from 0 to 127, all different within a row; in each aligned block of 16 rows (0 to 15, 16 to 31, ...) at most 2 rows name the same one
- affinity: float32 [2048, 8], P(('dp', 'tp')), may hold values from 0.05 to 1
Outputs:
- layer_out: bfloat16 [2048, 3584], P(('dp', 'tp'))
Inputs may be any that keep to these rules, and one draw needn't show every extreme that they name: `expert_ids`: in each aligned block of 16 rows (the rows of one device) no expert is named by more than 2 rows.
All inputs are finite; a program needn't handle non-finite values.
Results may differ from a plain program's by a relative error of at most 0.0081.
Values may be sent and summed in bfloat16 or wider, within the bound.
A program may use at most 128 MiB of HBM per device.

v0:
```python
import jax
import jax.numpy as jnp
from jax import lax
from jax.sharding import PartitionSpec as P

score_scale = 192.0 ** (-0.5)
norm_eps = 1e-06
route_scale = 2.5


def in_blocks(shard, dim, peers):
    before, after = (shard.shape[:dim], shard.shape[dim + 1 :])
    return jnp.moveaxis(shard.reshape(*before, peers, -1, *after), dim, 0)


def sum_at_owner(shard, axis, dim):
    peers = lax.axis_size(axis)
    parts = lax.all_to_all(in_blocks(shard, dim, peers), axis, 0, 0, tiled=True)
    return jnp.sum(parts.astype(jnp.float32), axis=0)


def attend(query_latent, query_rope, cache_latent, cache_rope, lengths):
    token_count, head_count, latent_width = query_latent.shape
    rope_width = cache_rope.shape[1]
    context = cache_latent.shape[1]
    query_rot = query_rope.reshape(token_count, head_count, rope_width)
    scores = jnp.einsum(
        "thl,tpl->thp", query_latent, cache_latent, preferred_element_type=jnp.float32
    )
    scores = scores + jnp.einsum(
        "thr,trp->thp", query_rot, cache_rope, preferred_element_type=jnp.float32
    )
    scores = scores * score_scale
    position = lax.broadcasted_iota(jnp.int32, (token_count, 1, context), 2)
    scores = jnp.where(position < lengths[:, None, None], scores, -jnp.inf)
    row_max = jnp.max(scores, axis=2, keepdims=True)
    raised = jnp.exp(scores - row_max)
    attn_weights = (raised / jnp.sum(raised, axis=2, keepdims=True)).astype(jnp.bfloat16)
    latent_out = jnp.einsum(
        "thp,tpl->thl", attn_weights, cache_latent, preferred_element_type=jnp.float32
    )
    return latent_out.astype(jnp.bfloat16)


def per_device(
    hidden_in,
    query_latent,
    query_rope,
    cache_latent,
    cache_rope,
    lengths,
    value_up,
    out_proj,
    norm_gain,
    expert_gate,
    expert_down,
    expert_ids,
    affinity,
):
    latent_out = attend(query_latent, query_rope, cache_latent, cache_rope, lengths)
    group_size = lax.axis_size("tp")
    local_heads = latent_out.shape[1] // group_size
    by_heads = lax.all_to_all(latent_out, "tp", split_axis=1, concat_axis=0, tiled=True)
    head_width = value_up.shape[1] // local_heads
    up_table = value_up.reshape(value_up.shape[0], local_heads, head_width)
    per_head = jnp.einsum(
        "thl,lhv->thv", by_heads, up_table, preferred_element_type=jnp.float32
    ).astype(jnp.bfloat16)
    attn_sum = sum_at_owner(
        jnp.dot(
            per_head.reshape(hidden_in.shape[0] * lax.axis_size("tp"), local_heads * head_width),
            out_proj,
            preferred_element_type=jnp.float32,
        ).astype(jnp.bfloat16),
        "tp",
        0,
    )
    hidden = (hidden_in.astype(jnp.float32) + attn_sum).astype(jnp.bfloat16)
    wide_hidden = hidden.astype(jnp.float32)
    inv_norm = lax.rsqrt(jnp.mean(wide_hidden * wide_hidden, axis=1, keepdims=True) + norm_eps)
    normed = (wide_hidden * inv_norm * norm_gain).astype(jnp.bfloat16)
    tok_rows, top_count = expert_ids.shape
    width = normed.shape[1]
    experts = expert_gate.shape[0] * lax.axis_size("dp") * lax.axis_size("tp")
    capacity = max(2, -(-(tok_rows * top_count) // experts))
    flat_ids = expert_ids.reshape(-1)
    expert_iota = lax.broadcasted_iota(jnp.int32, (1, experts), 1)
    one_hot = (flat_ids[:, None] == expert_iota).astype(jnp.int32)
    earlier = jnp.cumsum(one_hot, axis=0) - one_hot
    slot_index = jnp.sum(earlier * one_hot, axis=1)
    target = flat_ids * capacity + slot_index
    owner_row = jnp.arange(tok_rows * top_count, dtype=jnp.int32) // top_count
    source_row = jnp.full((experts * capacity,), tok_rows, jnp.int32).at[target].set(owner_row)
    padded = jnp.concatenate([normed, jnp.zeros((1, width), jnp.bfloat16)], axis=0)
    outgoing = padded[source_row].reshape(experts, capacity, width)
    gate_local = expert_gate[0]
    down_local = expert_down[0]
    slot_rows = lax.all_to_all(outgoing, ("dp", "tp"), split_axis=0, concat_axis=0, tiled=True)
    lead_shape = slot_rows.shape[:-1]
    flat_rows = slot_rows.reshape(-1, width)
    inner_act = jax.nn.silu(
        jnp.dot(flat_rows, gate_local, preferred_element_type=jnp.float32)
    ).astype(jnp.bfloat16)
    answer = jnp.dot(inner_act, down_local, preferred_element_type=jnp.float32).astype(jnp.bfloat16)
    answered = answer.reshape(lead_shape + (width,))
    returned = lax.all_to_all(answered, ("dp", "tp"), split_axis=0, concat_axis=0, tiled=True)
    returned = returned.reshape(experts * capacity, width)
    picked = returned[target].reshape(tok_rows, top_count, width).astype(jnp.float32)
    route_weight = route_scale * affinity / jnp.sum(affinity, axis=1, keepdims=True)
    moe_sum = jnp.sum(picked * route_weight[:, :, None], axis=1)
    return (wide_hidden + moe_sum).astype(jnp.bfloat16)


def solution(mesh):
    return jax.shard_map(
        per_device,
        mesh=mesh,
        in_specs=(
            P(("dp", "tp"), None),
            P(("dp", "tp"), None, None),
            P(("dp", "tp"), None),
            P(("dp", "tp"), None, None),
            P(("dp", "tp"), None, None),
            P(("dp", "tp")),
            P(None, "tp"),
            P("tp", None),
            P(),
            P(("dp", "tp"), None, None),
            P(("dp", "tp"), None, None),
            P(("dp", "tp"), None),
            P(("dp", "tp"), None),
        ),
        out_specs=P(("dp", "tp"), None),
        check_vma=False,
    )
```

profile of v0, /device:TPU:1, one launch (start us, length us, event | category | flops | bytes accessed | tf_op | source)
XLA Modules:
  0.0 159.0 jit_solution(15531151931945262616)
XLA Ops:
  0.0 1.3 reshape.88
  1.3 0.7 iota_compare_fusion.1
  2.1 1.2 fusion.31
  3.2 2.1 %fusion.12 = f32[16,64,128]{2,1,0:T(8,128)S(1)} fusion(f32[16,64,128]{2,1,0:T(8,128)S(1)} %fusion.31, bf16[16,64,512]{2,1,0:T(8,128)(2,1)} %param.14, bf16[16,128,512]{2,1,0:T(8,128)(2,1)S(1)} %copy-done, pred[16,128]{1,0:T(8,128)(4,1)S(1)} %iota_compare_fusion.1), kind=kOutput, calls=%fused_computation.17 | convolution fusion | flops 134610944 | bytes 4196352 | tf_op jit(solution)/shard_map/thl,tpl->thp/dot_general | solution.py:27
  5.3 0.3 fusion.30
  5.7 3.0 %convolution_convert_fusion.1 = bf16[16,64,512]{2,1,0:T(8,128)(2,1)} fusion(bf16[16,128,512]{2,1,0:T(8,128)(2,1)S(1)} %copy-done, f32[16,64]{1,0:T(8,128)S(1)} %fusion.30, f32[16,64,128]{2,1,0:T(8,128)S(1)} %fusion.12), kind=kOutput, calls=%fused_computation.12 | convolution fusion | flops 135136384 | bytes 3674112 | tf_op jit(solution)/shard_map/thp,tpl->thl/dot_general | solution.py:39
  8.6 2.8 %copy.25 = bf16[16,64,512]{2,0,1:T(8,128)(2,1)} copy(bf16[16,64,512]{2,1,0:T(8,128)(2,1)} %convolution_convert_fusion.1) | data formatting | bytes 2097152 | tf_op jit(solution)/shard_map/convert_element_type | solution.py:42
  11.4 5.1 %all-to-all-start = ((bf16[16,64,512]{2,0,1:T(8,128)(2,1)}), bf16[16,64,512]{2,0,1:T(8,128)(2,1)S(1)}, u32[]{:S(2)}, u32[]{:S(2)}) async-start(bf16[16,64,512]{2,0,1:T(8,128)(2,1)} %copy.25), calls=%async_computation | async-start | bytes 2097152 | tf_op jit(solution)/shard_map/all_to_all | solution.py:63
  16.6 2.3 %copy.27 = bf16[512,1024]{0,1:T(8,128)(2,1)} copy(bf16[512,1024]{1,0:T(8,128)(2,1)} %param.19) | data formatting | bytes 2097152 | tf_op args[6]
  19.3 0.2 reduce_window_sum.11
  19.4 0.2 select_reduce_fusion
  19.6 11.2 %all-to-all-done = bf16[16,64,512]{2,0,1:T(8,128)(2,1)S(1)} async-done(((bf16[16,64,512]{2,0,1:T(8,128)(2,1)}), bf16[16,64,512]{2,0,1:T(8,128)(2,1)S(1)}, u32[]{:S(2)}, u32[]{:S(2)}) %all-to-all-start) | async-done | bytes 1048608 | tf_op jit(solution)/shard_map/all_to_all | solution.py:63
  30.9 1.1 copy-done.1
  32.0 0.4 fusion.13
  32.4 0.2 copy.28
  32.6 0.2 reshape.90
  32.8 5.3 %convolution_convert_fusion = bf16[64,3584]{1,0:T(8,128)(2,1)} fusion(bf16[64,1024]{1,0:T(8,128)(2,1)S(1)} %reshape.90, bf16[1024,3584]{1,0:T(8,128)(2,1)} %param.20), kind=kOutput, calls=%fused_computation.9 | convolution fusion | flops 469991424 | bytes 7929856 | tf_op jit(solution)/shard_map/dot_general | solution.py:70
  38.1 3.5 %all-to-all-start.1 = ((bf16[4,16,3584]{2,1,0:T(8,128)(2,1)}), bf16[4,16,3584]{2,1,0:T(8,128)(2,1)S(1)}, u32[]{:S(2)}, u32[]{:S(2)}) async-start(bf16[4,16,3584]{2,1,0:T(8,128)(2,1)} %bitcast.5), calls=%async_computation.1 | async-start | bytes 917504 | tf_op jit(solution)/shard_map/all_to_all | solution.py:18
  41.6 1.0 scatter_custom_fusion
  42.6 5.7 %all-to-all-done.1 = bf16[4,16,3584]{2,1,0:T(8,128)(2,1)S(1)} async-done(((bf16[4,16,3584]{2,1,0:T(8,128)(2,1)}), bf16[4,16,3584]{2,1,0:T(8,128)(2,1)S(1)}, u32[]{:S(2)}, u32[]{:S(2)}) %all-to-all-start.1) | async-done | bytes 458784 | tf_op jit(solution)/shard_map/all_to_all | solution.py:18
  48.7 2.9 %gather_fusion = bf16[256,3584]{1,0:T(8,128)(2,1)} fusion(bf16[17,3584]{1,0:T(8,128)(2,1)S(1)} %concatenate.3, s32[1024]{0:T(1024)S(1)} %pad_clamp_fusion.1), kind=kCustom, calls=%fused_computation | custom fusion | bytes 3671040 | tf_op jit(solution)/shard_map/gather | solution.py:95
  51.6 4.8 %reshape.92 = bf16[128,2,3584]{2,1,0:T(2,128)(2,1)} reshape(bf16[256,3584]{1,0:T(8,128)(2,1)} %gather_fusion) | data formatting | bytes 3670016 | tf_op jit(solution)/shard_map/reshape | solution.py:95
  56.4 39.2 %all_to_all.33 = bf16[128,2,3584]{2,1,0:T(2,128)(2,1)} all-to-all(bf16[128,2,3584]{2,1,0:T(2,128)(2,1)} %reshape.92), channel_id=1, replica_groups=mesh['dp'=32,'tp'=4] {'dp','tp'}, dimensions={0} | all-to-all | bytes 3670016 | tf_op jit(solution)/shard_map/all_to_all | solution.py:98
  95.7 5.0 %reshape.93 = bf16[256,3584]{1,0:T(8,128)(2,1)} reshape(bf16[128,2,3584]{2,1,0:T(2,128)(2,1)} %all_to_all.33) | data formatting | bytes 3670016 | tf_op jit(solution)/shard_map/reshape | solution.py:100
  100.6 10.9 %fusion.5 = bf16[256,3584]{1,0:T(8,128)(2,1)} fusion(bf16[1,1024,3584]{2,1,0:T(8,128)(2,1)} %param.23, bf16[256,3584]{1,0:T(8,128)(2,1)} %reshape.93, bf16[1,3584,1024]{2,1,0:T(8,128)(2,1)} %param.22), kind=kOutput, calls=%fused_computation.8 | convolution fusion | flops 3760324608 | bytes 18350080 | tf_op jit(solution)/shard_map/dot_general | solution.py:104
  111.5 4.8 %reshape.94 = bf16[128,2,3584]{2,1,0:T(2,128)(2,1)} reshape(bf16[256,3584]{1,0:T(8,128)(2,1)} %fusion.5) | data formatting | bytes 3670016 | tf_op jit(solution)/shard_map/reshape | solution.py:105
  116.3 4.8 %all-to-all-start.3 = ((bf16[128,2,3584]{2,1,0:T(2,128)(2,1)}), bf16[128,2,3584]{2,1,0:T(2,128)(2,1)}, u32[]{:S(2)}, u32[]{:S(2)}) async-start(bf16[128,2,3584]{2,1,0:T(2,128)(2,1)} %reshape.94), calls=%async_computation.3 | async-start | bytes 3670016 | tf_op jit(solution)/shard_map/all_to_all | solution.py:106
  121.2 27.8 %all-to-all-done.3 = bf16[128,2,3584]{2,1,0:T(2,128)(2,1)} async-done(((bf16[128,2,3584]{2,1,0:T(2,128)(2,1)}), bf16[128,2,3584]{2,1,0:T(2,128)(2,1)}, u32[]{:S(2)}, u32[]{:S(2)}) %all-to-all-start.3) | async-done | bytes 1835040 | tf_op jit(solution)/shard_map/all_to_all | solution.py:106
  149.0 4.9 %reshape.95 = bf16[256,3584]{1,0:T(8,128)(2,1)} reshape(bf16[128,2,3584]{2,1,0:T(2,128)(2,1)} %all-to-all-done.3) | data formatting | bytes 3670016 | tf_op jit(solution)/shard_map/reshape | solution.py:107
  153.9 3.8 %gather_fusion.1 = bf16[128,3584]{1,0:T(8,128)(2,1)S(1)} fusion(bf16[256,3584]{1,0:T(8,128)(2,1)} %reshape.95, s32[1024]{0:T(1024)S(1)} %pad_clamp_fusion), kind=kCustom, calls=%fused_computation.1 | custom fusion | bytes 1835520 | tf_op jit(solution)/shard_map/gather | solution.py:108
  157.7 0.7 fusion.8
  158.3 0.7 fusion.23
  (31 shorter events, 1.0 us)
Async XLA Ops:
  0.0 3.2 %copy-start = (bf16[16,128,512]{2,1,0:T(8,128)(2,1)S(1)}, bf16[16,128,512]{2,1,0:T(8,128)(2,1)}, u32[]{:S(2)}) copy-start(bf16[16,128,512]{2,1,0:T(8,128)(2,1)} %param.16) | copy-start | bytes 6291460
  11.4 7.4 %copy-start.3 = (s32[16,8]{0,1:T(8,128)S(1)}, s32[16,8]{0,1:T(8,128)}, u32[]{:S(2)}) copy-start(s32[16,8]{0,1:T(8,128)} %param.24) | copy-start | bytes 1540
  11.4 19.4 %all-to-all-start = ((bf16[16,64,512]{2,0,1:T(8,128)(2,1)}), bf16[16,64,512]{2,0,1:T(8,128)(2,1)S(1)}, u32[]{:S(2)}, u32[]{:S(2)}) async-start(bf16[16,64,512]{2,0,1:T(8,128)(2,1)} %copy.25), calls=%async_computation | async-start | bytes 2097152 | tf_op jit(solution)/shard_map/all_to_all | solution.py:63
  30.8 1.2 copy-start.1
  32.8 15.6 %copy-start.2 = (bf16[16,3584]{1,0:T(8,128)(2,1)S(1)}, bf16[16,3584]{1,0:T(8,128)(2,1)}, u32[]{:S(2)}) copy-start(bf16[16,3584]{1,0:T(8,128)(2,1)} %param.13) | copy-start | bytes 344068
  32.8 15.7 %copy-start.5 = (f32[3584]{0:T(1024)S(1)}, f32[3584]{0:T(1024)}, u32[]{:S(2)}) copy-start(f32[3584]{0:T(1024)} %param.21) | copy-start | bytes 43012
  38.1 10.2 %all-to-all-start.1 = ((bf16[4,16,3584]{2,1,0:T(8,128)(2,1)}), bf16[4,16,3584]{2,1,0:T(8,128)(2,1)S(1)}, u32[]{:S(2)}, u32[]{:S(2)}) async-start(bf16[4,16,3584]{2,1,0:T(8,128)(2,1)} %bitcast.5), calls=%async_computation.1 | async-start | bytes 917504 | tf_op jit(solution)/shard_map/all_to_all | solution.py:18
  116.3 4.8 %copy-start.4 = (f32[16,8]{0,1:T(8,128)S(1)}, f32[16,8]{0,1:T(8,128)}, u32[]{:S(2)}) copy-start(f32[16,8]{0,1:T(8,128)} %param.25) | copy-start | bytes 1540
  116.3 32.7 %all-to-all-start.3 = ((bf16[128,2,3584]{2,1,0:T(2,128)(2,1)}), bf16[128,2,3584]{2,1,0:T(2,128)(2,1)}, u32[]{:S(2)}, u32[]{:S(2)}) async-start(bf16[128,2,3584]{2,1,0:T(2,128)(2,1)} %reshape.94), calls=%async_computation.3 | async-start | bytes 3670016 | tf_op jit(solution)/shard_map/all_to_all | solution.py:106
where the time goes:
time: 160 us; the launch traced here: 159 us
  waiting for transfers between devices  44.7 us (28%)
  blocking collectives  39.2 us (25%)
  local copies, waits for them, and re-layouts  35.5 us (22%)
  matrix products  22.8 us (14%)
  starting transfers between devices  13.4 us (8%)
  other arithmetic  3.25 us (2%)
    all_to_all x1, blocking collectives, per_device(): lax.all_to_all(outgoing, ('dp', 'tp'), split_axis=0, concat_axis=0, tiled...  39.2 us
    all_to_all x1, waiting for transfers between devices, per_device(): lax.all_to_all(answered, ('dp', 'tp'), split_axis=0, concat_axis=0, tiled...  27.8 us
    all_to_all x1, waiting for transfers between devices, per_device(): lax.all_to_all(latent_out, 'tp', split_axis=1, concat_axis=0, tiled=True)  11.2 us
    dot_general x1, matrix products, per_device(): jnp.dot(inner_act, down_local, preferred_element_type=jnp.float32)  10.9 us
    all_to_all x1, waiting for transfers between devices, sum_at_owner(): parts = lax.all_to_all(in_blocks(shard, dim, peers), axis, 0, 0, tiled=True)  5.71 us
    dot_general x1, matrix products, per_device(): jnp.dot(per_head.reshape(hidden_in.shape[0] * lax.axis_size('tp'), local_...  5.27 us
    all_to_all x1, starting transfers between devices, per_device(): lax.all_to_all(latent_out, 'tp', split_axis=1, concat_axis=0, tiled=True)  5.14 us
    reshape x1, local copies, waits for them, and re-layouts, per_device(): flat_rows = slot_rows.reshape(-1, width)  4.95 us
  transfers between devices with their start and end apart: 3, of which 3 were waited for; matrix products, arithmetic and copies ran while one was open for 3% of the time, Pallas kernels for 0%

commit v1 on v0

--- a/solution.py
+++ b/solution.py
@@ -60,7 +60,10 @@
     latent_out = attend(query_latent, query_rope, cache_latent, cache_rope, lengths)
     group_size = lax.axis_size("tp")
     local_heads = latent_out.shape[1] // group_size
-    by_heads = lax.all_to_all(latent_out, "tp", split_axis=1, concat_axis=0, tiled=True)
+    by_heads = jnp.concatenate(
+        lax.all_to_all(jnp.stack(jnp.split(latent_out, lax.axis_size("tp"), axis=1)), "tp", 0, 0),
+        axis=0,
+    )
     head_width = value_up.shape[1] // local_heads
     up_table = value_up.reshape(value_up.shape[0], local_heads, head_width)
     per_head = jnp.einsum(

time: 160 us -> 160 us (level)
  local copies, waits for them, and re-layouts: 35.5 us -> 31.8 us
  matrix products: 22.8 us -> 24.6 us
    convert_element_type x1 -> x0, local copies, waits for them, and re-layouts: 2.79 us -> none  [attend(): return latent_out.astype(jnp.bfloat16)]
    unnamed x14, local copies, waits for them, and re-layouts: 3.52 us -> 1.44 us
    dot_general x1, matrix products: 0.41 us -> 2.28 us  [per_device(): jnp.einsum('thl,lhv->thv', by_heads, up_table, preferred_element_type=jnp...]
  transfers between devices with their start and end apart: 3 -> 3, of which waited for: 3 -> 3; matrix products, arithmetic and copies ran while one was open for 3% -> 2% of each run, Pallas kernels for 0% -> 0%
where the time goes in v1:
time: 160 us; the launch traced here: 159 us
  waiting for transfers between devices  45.7 us (29%)
  blocking collectives  39.3 us (25%)
  local copies, waits for them, and re-layouts  31.8 us (20%)
  matrix products  24.6 us (15%)
  starting transfers between devices  13.4 us (8%)
  other arithmetic  4.36 us (3%)
    all_to_all x1, blocking collectives, per_device(): lax.all_to_all(outgoing, ('dp', 'tp'), split_axis=0, concat_axis=0, tiled...  39.3 us
    all_to_all x1, waiting for transfers between devices, per_device(): lax.all_to_all(answered, ('dp', 'tp'), split_axis=0, concat_axis=0, tiled...  27.8 us
    all_to_all x1, waiting for transfers between devices, per_device(): lax.all_to_all(jnp.stack(jnp.split(latent_out, lax.axis_size('tp'), axis=...  12.2 us
    dot_general x1, matrix products, per_device(): jnp.dot(inner_act, down_local, preferred_element_type=jnp.float32)  10.9 us
    all_to_all x1, waiting for transfers between devices, sum_at_owner(): parts = lax.all_to_all(in_blocks(shard, dim, peers), axis, 0, 0, tiled=True)  5.71 us
    dot_general x1, matrix products, per_device(): jnp.dot(per_head.reshape(hidden_in.shape[0] * lax.axis_size('tp'), local_...  5.27 us
    all_to_all x1, starting transfers between devices, per_device(): lax.all_to_all(jnp.stack(jnp.split(latent_out, lax.axis_size('tp'), axis=...  5.14 us
    reshape x1, local copies, waits for them, and re-layouts, per_device(): flat_rows = slot_rows.reshape(-1, width)  4.95 us
  transfers between devices with their start and end apart: 3, of which 3 were waited for; matrix products, arithmetic and copies ran while one was open for 2% of the time, Pallas kernels for 0%

profile of v1, /device:TPU:1, one launch (start us, length us, event | category | flops | bytes accessed | tf_op | source)
XLA Modules:
  0.0 159.4 jit_solution(5665166618368844681)
XLA Ops:
  0.0 1.3 reshape.91
  1.3 0.7 iota_compare_fusion.1
  2.1 1.2 fusion.32
  3.2 2.1 %fusion.12 = f32[16,64,128]{2,1,0:T(8,128)S(1)} fusion(f32[16,64,128]{2,1,0:T(8,128)S(1)} %fusion.32, bf16[16,64,512]{2,1,0:T(8,128)(2,1)} %param.14, bf16[16,128,512]{2,1,0:T(8,128)(2,1)S(1)} %copy-done, pred[16,128]{1,0:T(8,128)(4,1)S(1)} %iota_compare_fusion.1), kind=kOutput, calls=%fused_computation.17 | convolution fusion | flops 134610944 | bytes 4196352 | tf_op jit(solution)/shard_map/thl,tpl->thp/dot_general | solution.py:27
  5.3 0.3 fusion.31
  5.7 2.9 %convolution_convert_fusion.1 = bf16[16,64,512]{2,1,0:T(8,128)(2,1)} fusion(bf16[16,128,512]{2,1,0:T(8,128)(2,1)S(1)} %copy-done, f32[16,64]{1,0:T(8,128)S(1)} %fusion.31, f32[16,64,128]{2,1,0:T(8,128)S(1)} %fusion.12), kind=kOutput, calls=%fused_computation.12 | convolution fusion | flops 135136384 | bytes 3674112 | tf_op jit(solution)/shard_map/thp,tpl->thl/dot_general | solution.py:39
  8.6 1.3 slice_bitcast_fusion.3
  9.9 1.1 pad_maximum_fusion
  11.0 5.1 %all-to-all-start = ((bf16[4,16,16,512]{3,2,1,0:T(8,128)(2,1)}), bf16[4,16,16,512]{3,2,1,0:T(8,128)(2,1)}, u32[]{:S(2)}, u32[]{:S(2)}) async-start(bf16[4,16,16,512]{3,2,1,0:T(8,128)(2,1)} %pad_maximum_fusion), calls=%async_computation | async-start | bytes 2097152 | tf_op jit(solution)/shard_map/all_to_all | solution.py:64
  16.1 1.3 copy.19
  17.9 0.2 reduce_window_sum.11
  18.0 0.2 select_reduce_fusion
  18.2 12.2 %all-to-all-done = bf16[4,16,16,512]{3,2,1,0:T(8,128)(2,1)} async-done(((bf16[4,16,16,512]{3,2,1,0:T(8,128)(2,1)}), bf16[4,16,16,512]{3,2,1,0:T(8,128)(2,1)}, u32[]{:S(2)}, u32[]{:S(2)}) %all-to-all-start) | async-done | bytes 1048608 | tf_op jit(solution)/shard_map/all_to_all | solution.py:64
  30.5 2.3 %fusion.13 = bf16[64,16,64]{2,0,1:T(8,128)(2,1)S(1)} fusion(bf16[512,16,64]{0,2,1:T(8,128)(2,1)} %bitcast.45, bf16[64,16,512]{2,1,0:T(8,128)(2,1)} %bitcast.4), kind=kOutput, calls=%fused_computation.19 | convolution fusion | flops 67174400 | bytes 2228224 | tf_op jit(solution)/shard_map/thl,lhv->thv/dot_general | solution.py:69
  32.7 0.2 copy.21
  32.9 0.2 reshape.94
  33.1 5.3 %convolution_convert_fusion = bf16[64,3584]{1,0:T(8,128)(2,1)} fusion(bf16[64,1024]{1,0:T(8,128)(2,1)S(1)} %reshape.94, bf16[1024,3584]{1,0:T(8,128)(2,1)} %param.20), kind=kOutput, calls=%fused_computation.9 | convolution fusion | flops 469991424 | bytes 7929856 | tf_op jit(solution)/shard_map/dot_general | solution.py:73
  38.4 3.5 %all-to-all-start.1 = ((bf16[4,16,3584]{2,1,0:T(8,128)(2,1)}), bf16[4,16,3584]{2,1,0:T(8,128)(2,1)S(1)}, u32[]{:S(2)}, u32[]{:S(2)}) async-start(bf16[4,16,3584]{2,1,0:T(8,128)(2,1)} %bitcast.7), calls=%async_computation.1 | async-start | bytes 917504 | tf_op jit(solution)/shard_map/all_to_all | solution.py:18
  41.9 1.0 scatter_custom_fusion
  42.9 5.7 %all-to-all-done.1 = bf16[4,16,3584]{2,1,0:T(8,128)(2,1)S(1)} async-done(((bf16[4,16,3584]{2,1,0:T(8,128)(2,1)}), bf16[4,16,3584]{2,1,0:T(8,128)(2,1)S(1)}, u32[]{:S(2)}, u32[]{:S(2)}) %all-to-all-start.1) | async-done | bytes 458784 | tf_op jit(solution)/shard_map/all_to_all | solution.py:18
  49.0 2.9 %gather_fusion = bf16[256,3584]{1,0:T(8,128)(2,1)} fusion(bf16[17,3584]{1,0:T(8,128)(2,1)S(1)} %concatenate.3, s32[1024]{0:T(1024)S(1)} %pad_clamp_fusion.1), kind=kCustom, calls=%fused_computation | custom fusion | bytes 3671040 | tf_op jit(solution)/shard_map/gather | solution.py:98
  51.9 4.8 %reshape.96 = bf16[128,2,3584]{2,1,0:T(2,128)(2,1)} reshape(bf16[256,3584]{1,0:T(8,128)(2,1)} %gather_fusion) | data formatting | bytes 3670016 | tf_op jit(solution)/shard_map/reshape | solution.py:98
  56.7 39.3 %all_to_all.20 = bf16[128,2,3584]{2,1,0:T(2,128)(2,1)} all-to-all(bf16[128,2,3584]{2,1,0:T(2,128)(2,1)} %reshape.96), channel_id=1, replica_groups=mesh['dp'=32,'tp'=4] {'dp','tp'}, dimensions={0} | all-to-all | bytes 3670016 | tf_op jit(solution)/shard_map/all_to_all | solution.py:101
  96.0 5.0 %reshape.97 = bf16[256,3584]{1,0:T(8,128)(2,1)} reshape(bf16[128,2,3584]{2,1,0:T(2,128)(2,1)} %all_to_all.20) | data formatting | bytes 3670016 | tf_op jit(solution)/shard_map/reshape | solution.py:103
  101.0 10.9 %fusion.5 = bf16[256,3584]{1,0:T(8,128)(2,1)} fusion(bf16[1,1024,3584]{2,1,0:T(8,128)(2,1)} %param.23, bf16[256,3584]{1,0:T(8,128)(2,1)} %reshape.97, bf16[1,3584,1024]{2,1,0:T(8,128)(2,1)} %param.22), kind=kOutput, calls=%fused_computation.8 | convolution fusion | flops 3760324608 | bytes 18350080 | tf_op jit(solution)/shard_map/dot_general | solution.py:107
  111.8 4.8 %reshape.98 = bf16[128,2,3584]{2,1,0:T(2,128)(2,1)} reshape(bf16[256,3584]{1,0:T(8,128)(2,1)} %fusion.5) | data formatting | bytes 3670016 | tf_op jit(solution)/shard_map/reshape | solution.py:108
  116.6 4.8 %all-to-all-start.3 = ((bf16[128,2,3584]{2,1,0:T(2,128)(2,1)}), bf16[128,2,3584]{2,1,0:T(2,128)(2,1)}, u32[]{:S(2)}, u32[]{:S(2)}) async-start(bf16[128,2,3584]{2,1,0:T(2,128)(2,1)} %reshape.98), calls=%async_computation.3 | async-start | bytes 3670016 | tf_op jit(solution)/shard_map/all_to_all | solution.py:109
  121.5 27.8 %all-to-all-done.3 = bf16[128,2,3584]{2,1,0:T(2,128)(2,1)} async-done(((bf16[128,2,3584]{2,1,0:T(2,128)(2,1)}), bf16[128,2,3584]{2,1,0:T(2,128)(2,1)}, u32[]{:S(2)}, u32[]{:S(2)}) %all-to-all-start.3) | async-done | bytes 1835040 | tf_op jit(solution)/shard_map/all_to_all | solution.py:109
  149.3 4.9 %reshape.99 = bf16[256,3584]{1,0:T(8,128)(2,1)} reshape(bf16[128,2,3584]{2,1,0:T(2,128)(2,1)} %all-to-all-done.3) | data formatting | bytes 3670016 | tf_op jit(solution)/shard_map/reshape | solution.py:110
  154.2 3.8 %gather_fusion.1 = bf16[128,3584]{1,0:T(8,128)(2,1)S(1)} fusion(bf16[256,3584]{1,0:T(8,128)(2,1)} %reshape.99, s32[1024]{0:T(1024)S(1)} %pad_clamp_fusion), kind=kCustom, calls=%fused_computation.1 | custom fusion | bytes 1835520 | tf_op jit(solution)/shard_map/gather | solution.py:111
  158.0 0.7 fusion.8
  158.7 0.7 fusion.24
  (31 shorter events, 0.9 us)
Async XLA Ops:
  0.0 3.2 %copy-start = (bf16[16,128,512]{2,1,0:T(8,128)(2,1)S(1)}, bf16[16,128,512]{2,1,0:T(8,128)(2,1)}, u32[]{:S(2)}) copy-start(bf16[16,128,512]{2,1,0:T(8,128)(2,1)} %param.16) | copy-start | bytes 6291460
  9.8 6.3 %copy-start.1 = (bf16[512,1024]{1,0:T(8,128)(2,1)S(1)}, bf16[512,1024]{1,0:T(8,128)(2,1)}, u32[]{:S(2)}) copy-start(bf16[512,1024]{1,0:T(8,128)(2,1)} %param.19) | copy-start | bytes 3145732
  11.0 6.5 %copy-start.3 = (s32[16,8]{0,1:T(8,128)S(1)}, s32[16,8]{0,1:T(8,128)}, u32[]{:S(2)}) copy-start(s32[16,8]{0,1:T(8,128)} %param.24) | copy-start | bytes 1540
  11.0 19.5 %all-to-all-start = ((bf16[4,16,16,512]{3,2,1,0:T(8,128)(2,1)}), bf16[4,16,16,512]{3,2,1,0:T(8,128)(2,1)}, u32[]{:S(2)}, u32[]{:S(2)}) async-start(bf16[4,16,16,512]{3,2,1,0:T(8,128)(2,1)} %pad_maximum_fusion), calls=%async_computation | async-start | bytes 2097152 | tf_op jit(solution)/shard_map/all_to_all | solution.py:64
  33.1 15.6 %copy-start.2 = (bf16[16,3584]{1,0:T(8,128)(2,1)S(1)}, bf16[16,3584]{1,0:T(8,128)(2,1)}, u32[]{:S(2)}) copy-start(bf16[16,3584]{1,0:T(8,128)(2,1)} %param.13) | copy-start | bytes 344068
  33.1 15.7 %copy-start.5 = (f32[3584]{0:T(1024)S(1)}, f32[3584]{0:T(1024)}, u32[]{:S(2)}) copy-start(f32[3584]{0:T(1024)} %param.21) | copy-start | bytes 43012
  38.4 10.2 %all-to-all-start.1 = ((bf16[4,16,3584]{2,1,0:T(8,128)(2,1)}), bf16[4,16,3584]{2,1,0:T(8,128)(2,1)S(1)}, u32[]{:S(2)}, u32[]{:S(2)}) async-start(bf16[4,16,3584]{2,1,0:T(8,128)(2,1)} %bitcast.7), calls=%async_computation.1 | async-start | bytes 917504 | tf_op jit(solution)/shard_map/all_to_all | solution.py:18
  116.6 4.8 %copy-start.4 = (f32[16,8]{0,1:T(8,128)S(1)}, f32[16,8]{0,1:T(8,128)}, u32[]{:S(2)}) copy-start(f32[16,8]{0,1:T(8,128)} %param.25) | copy-start | bytes 1540
  116.6 32.7 %all-to-all-start.3 = ((bf16[128,2,3584]{2,1,0:T(2,128)(2,1)}), bf16[128,2,3584]{2,1,0:T(2,128)(2,1)}, u32[]{:S(2)}, u32[]{:S(2)}) async-start(bf16[128,2,3584]{2,1,0:T(2,128)(2,1)} %reshape.98), calls=%async_computation.3 | async-start | bytes 3670016 | tf_op jit(solution)/shard_map/all_to_all | solution.py:109
